TPU v7x, 128 devices: a whole 4x4x4 slice. The times are simulated.
128 devices in a mesh: gen: 16 (over x, z_hi, core), tp: 8 (over y, z_lo).
Axes of the slice: x: 4, y: 4, z: 4 (z_hi: 2, z_lo: 2; z = z_hi * 2 + z_lo), core: 2. Of those that a mesh axis runs over, the one named last changes fastest.
Arguments:
- hidden_in: bfloat16 [4, 32, 8192], P(None, 'gen'), may hold values from -6 to 6
- norm_gain: bfloat16 [8192], replicated, may hold values from 0.099609375 to 1.8984375
- w_query: bfloat16 [8192, 4096], P(('gen', 'tp')), may hold values from -0.0625 to 0.0625
- key_weight_matrix: bfloat16 [8192, 1024], P(('gen', 'tp')), may hold values from -0.0625 to 0.0625
- value_weight_matrix: bfloat16 [8192, 1024], P(('gen', 'tp')), may hold values from -0.0625 to 0.0625
- bias_query: bfloat16 [4096], P('tp'), may hold values from -3 to 3
- key_bias_vector: bfloat16 [1024], P('tp'), may hold values from -3 to 3
- value_bias_vector: bfloat16 [1024], P('tp'), may hold values from -3 to 3
- w_out: bfloat16 [4096, 8192], P(None, ('gen', 'tp')), may hold values from -0.09375 to 0.09375
- key_cache: bfloat16 [32, 8, 16384, 128], P('gen', 'tp'), may hold values from -400 to 400
- value_cache: bfloat16 [32, 8, 16384, 128], P('gen', 'tp'), may hold values from -16 to 16
- lengths: int32 [32], P('gen'), may hold values from 1 to 16384
- finished: int32 [32], P('gen'), may hold values 0 or 1
Outputs:
- layer_out: bfloat16 [4, 32, 8192], P(None, 'gen')
All inputs are finite; a program needn't handle non-finite values. No bound on the sum of `finished` on one device may be relied on, other than what follows from the above.
Results may differ from a plain program's by a relative error of at most 0.012.
Values may be sent and summed in bfloat16 or wider, within the bound.
A program may use at most 128 MiB of HBM per device.

v0:
```python
import math
import jax
import jax.numpy as jnp
from jax import lax
from jax.sharding import PartitionSpec as P

norm_eps = 1e-06
rope_base = 1000000.0
masked_score = -1e30


def sent_together(arrays, axis, dim, along):
    widths = [a.shape[along] for a in arrays]
    both = jnp.concatenate(arrays, axis=along)
    filled = lax.all_gather(both, axis, axis=dim, tiled=True)
    return tuple(jnp.split(filled, [sum(widths[:k]) for k in range(1, len(widths))], axis=along))


def from_everyone(array, axis):
    copies = jnp.broadcast_to(array, (lax.axis_size(axis), *array.shape))
    return lax.all_to_all(copies, axis, split_axis=0, concat_axis=0, tiled=True)


def of_everyone(array, axis):
    return from_everyone(array, axis).astype(jnp.float32).sum(axis=0)


def apply_rotation(values, token_positions):
    half_dim = values.shape[-1] // 2
    pair_index = jnp.arange(half_dim).astype(jnp.float32)
    frequency = jnp.exp(pair_index * (-2.0 * math.log(rope_base) / values.shape[-1]))
    angles = token_positions[..., None] * frequency
    lower_half = values[..., :half_dim]
    upper_half = values[..., half_dim:]
    cosine = jnp.cos(angles)
    sine = jnp.sin(angles)
    return jnp.concatenate(
        [lower_half * cosine - upper_half * sine, upper_half * cosine + lower_half * sine], axis=-1
    )


def attend(queries, new_key_rows, fresh_value_rows, key_cache, value_cache, live_length):
    step_count, row_count, query_heads, head_dim = queries.shape
    kv_heads = new_key_rows.shape[2]
    group_size = query_heads // kv_heads
    cache_len = key_cache.shape[2]
    block_len = min(cache_len, 2048)
    score_scale = 1.0 / math.sqrt(head_dim)
    grouped_heads = queries.reshape(step_count, row_count, kv_heads, group_size, head_dim)
    grouped_heads = jnp.transpose(grouped_heads, (1, 2, 3, 0, 4)).reshape(
        row_count, kv_heads, group_size * step_count, head_dim
    )
    fresh_keys = jnp.transpose(new_key_rows, (1, 2, 0, 3))
    fresh_values = jnp.transpose(fresh_value_rows, (1, 2, 0, 3))
    fresh_scores = (
        jnp.einsum("rkqd,rkud->rkqu", grouped_heads, fresh_keys, preferred_element_type=jnp.float32)
        * score_scale
    )
    query_step = jnp.arange(group_size * step_count) % step_count
    allowed = jnp.arange(step_count)[None, :] <= query_step[:, None]
    fresh_scores = jnp.where(allowed, fresh_scores, masked_score)
    running_max = jnp.max(fresh_scores, axis=-1)
    weights = jnp.exp(fresh_scores - running_max[..., None])
    running_sum = jnp.sum(weights, axis=-1)
    numerator = jnp.einsum(
        "rkqu,rkud->rkqd",
        weights.astype(jnp.bfloat16),
        fresh_values,
        preferred_element_type=jnp.float32,
    )
    block_count = (jnp.max(live_length) + block_len - 1) // block_len

    def visit(block_index, carry):
        running_max, running_sum, numerator = carry
        key_block = lax.dynamic_slice_in_dim(key_cache, block_index * block_len, block_len, 2)
        value_block = lax.dynamic_slice_in_dim(value_cache, block_index * block_len, block_len, 2)
        scores = (
            jnp.einsum(
                "rkqd,rkcd->rkqc", grouped_heads, key_block, preferred_element_type=jnp.float32
            )
            * score_scale
        )
        places = block_index * block_len + jnp.arange(block_len)
        inside = places[None, :] < live_length[:, None]
        scores = jnp.where(inside[:, None, None, :], scores, masked_score)
        new_max = jnp.maximum(running_max, jnp.max(scores, axis=-1))
        factor = jnp.exp(running_max - new_max)
        weights = jnp.exp(scores - new_max[..., None])
        running_sum = running_sum * factor + jnp.sum(weights, axis=-1)
        numerator = numerator * factor[..., None] + jnp.einsum(
            "rkqc,rkcd->rkqd",
            weights.astype(jnp.bfloat16),
            value_block,
            preferred_element_type=jnp.float32,
        )
        return (new_max, running_sum, numerator)

    running_max, running_sum, numerator = lax.fori_loop(
        0, block_count, visit, (running_max, running_sum, numerator)
    )
    result = numerator / running_sum[..., None]
    result = result.reshape(row_count, kv_heads, group_size, step_count, head_dim)
    result = jnp.transpose(result, (3, 0, 1, 2, 4)).reshape(
        step_count, row_count, query_heads * head_dim
    )
    return result.astype(jnp.bfloat16)


def shards(
    hidden_in,
    norm_gain,
    w_query,
    key_weight_matrix,
    value_weight_matrix,
    bias_query,
    key_bias_vector,
    value_bias_vector,
    w_out,
    key_cache,
    value_cache,
    lengths,
    finished,
):
    step_count, row_count, model_width = hidden_in.shape
    head_dim = key_cache.shape[3]
    kv_heads = key_cache.shape[1]
    query_heads = bias_query.shape[0] // head_dim
    widened = hidden_in.astype(jnp.float32)
    normed = (
        widened
        * lax.rsqrt(jnp.mean(widened * widened, axis=-1, keepdims=True) + norm_eps)
        * norm_gain.astype(jnp.float32)
    )
    normed = normed.astype(jnp.bfloat16)
    flattened = normed.reshape(step_count * row_count, model_width)
    query_part, key_part, value_part = (
        lax.all_to_all(w_query, "tp", split_axis=1, concat_axis=0, tiled=True),
        lax.all_to_all(key_weight_matrix, "tp", split_axis=1, concat_axis=0, tiled=True),
        lax.all_to_all(value_weight_matrix, "tp", split_axis=1, concat_axis=0, tiled=True),
    )
    out_part = lax.all_to_all(w_out, "tp", split_axis=0, concat_axis=1, tiled=True)
    segments = sent_together((query_part, key_part, value_part), "gen", 0, 1)
    first_sum = jnp.dot(flattened, segments[0], preferred_element_type=jnp.float32)
    second_sum = jnp.dot(flattened, segments[1], preferred_element_type=jnp.float32)
    third_sum = jnp.dot(flattened, segments[2], preferred_element_type=jnp.float32)
    queries = first_sum
    new_key_rows = second_sum
    fresh_value_rows = third_sum
    queries = queries + bias_query.astype(jnp.float32)
    new_key_rows = new_key_rows + key_bias_vector.astype(jnp.float32)
    fresh_value_rows = fresh_value_rows + value_bias_vector.astype(jnp.float32)
    token_positions = (lengths[None, :] + jnp.arange(step_count, dtype=jnp.int32)[:, None]).astype(
        jnp.float32
    )[:, :, None]
    rot_query = apply_rotation(
        queries.reshape(step_count, row_count, query_heads, head_dim), token_positions
    ).astype(jnp.bfloat16)
    rotated_key = apply_rotation(
        new_key_rows.reshape(step_count, row_count, kv_heads, head_dim), token_positions
    ).astype(jnp.bfloat16)
    value_rows_new = fresh_value_rows.reshape(step_count, row_count, kv_heads, head_dim).astype(
        jnp.bfloat16
    )
    live_length = jnp.where(finished != 0, 0, lengths)
    attended = attend(rot_query, rotated_key, value_rows_new, key_cache, value_cache, live_length)
    attended_flat = attended.reshape(step_count * row_count, query_heads * head_dim)
    partial_out = jnp.dot(
        attended_flat,
        lax.all_gather(out_part, "gen", axis=1, tiled=True),
        preferred_element_type=jnp.float32,
    )
    projected = of_everyone(partial_out.astype(jnp.bfloat16), "tp").astype(jnp.float32)
    projected = projected.reshape(step_count, row_count, model_width)
    layer_out = jnp.where(finished[None, :, None] != 0, widened, widened + projected)
    return layer_out.astype(jnp.bfloat16)


def solution(mesh):
    placed = (
        P(None, "gen", None),
        P(),
        P(("gen", "tp"), None),
        P(("gen", "tp"), None),
        P(("gen", "tp"), None),
        P("tp"),
        P("tp"),
        P("tp"),
        P(None, ("gen", "tp")),
        P("gen", "tp", None, None),
        P("gen", "tp", None, None),
        P("gen"),
        P("gen"),
    )
    return jax.shard_map(
        shards, mesh=mesh, in_specs=placed, out_specs=P(None, "gen", None), check_vma=False
    )
```

profile of v0, /device:TPU:0, one launch (start us, length us, event | category | flops | bytes accessed | tf_op | source)
XLA Modules:
  0.0 241.8 jit_solution(11346730564790892831)
XLA Ops:
  6.6 1.0 copy-done
  7.5 0.7 copy_bitcast_fusion.3
  8.2 5.9 %all-to-all-start.1 = ((bf16[64,8,128]{2,0,1:T(8,128)(2,1)}), bf16[64,8,128]{2,0,1:T(8,128)(2,1)S(1)}, u32[]{:S(2)}, u32[]{:S(2)}) async-start(bf16[64,8,128]{2,0,1:T(8,128)(2,1)} %copy_bitcast_fusion.3), calls=%async_computation.1 | async-start | bytes 262144 | tf_op jit(solution)/shard_map/all_to_all | solution.py:138
  14.1 1.6 copy_bitcast_fusion.2
  15.7 4.8 %all-to-all-done.1 = bf16[64,8,128]{2,0,1:T(8,128)(2,1)S(1)} async-done(((bf16[64,8,128]{2,0,1:T(8,128)(2,1)}), bf16[64,8,128]{2,0,1:T(8,128)(2,1)S(1)}, u32[]{:S(2)}, u32[]{:S(2)}) %all-to-all-start.1) | async-done | bytes 131104 | tf_op jit(solution)/shard_map/all_to_all | solution.py:138
  20.5 3.4 %all-to-all-start.2 = ((bf16[64,8,128]{2,0,1:T(8,128)(2,1)}), bf16[64,8,128]{2,0,1:T(8,128)(2,1)S(1)}, u32[]{:S(2)}, u32[]{:S(2)}) async-start(bf16[64,8,128]{2,0,1:T(8,128)(2,1)} %copy_bitcast_fusion.2), calls=%async_computation.2 | async-start | bytes 262144 | tf_op jit(solution)/shard_map/all_to_all | solution.py:139
  23.9 0.0 all-gather.3.cloned.1.call-start
  24.0 1.1 copy.94
  25.1 5.2 %all-to-all-done.2 = bf16[64,8,128]{2,0,1:T(8,128)(2,1)S(1)} async-done(((bf16[64,8,128]{2,0,1:T(8,128)(2,1)}), bf16[64,8,128]{2,0,1:T(8,128)(2,1)S(1)}, u32[]{:S(2)}, u32[]{:S(2)}) %all-to-all-start.2) | async-done | bytes 131104 | tf_op jit(solution)/shard_map/all_to_all | solution.py:139
  30.3 11.0 %all_to_all.81 = bf16[64,8,512]{2,0,1:T(8,128)(2,1)S(1)} all-to-all(bf16[64,8,512]{2,0,1:T(8,128)(2,1)S(1)} %bitcast.117), channel_id=1, replica_groups=mesh['gen'=16,'tp'=8] {'tp'}, dimensions={1} | all-to-all | bytes 1048576 | tf_op jit(solution)/shard_map/all_to_all | solution.py:137
  41.3 1.0 pad_maximum_fusion
  42.2 0.0 all-gather.3.cloned.1.call-update
  42.3 0.0 all-gather.5.cloned.1.call-start
  42.3 1.1 copy.93
  43.4 11.4 %all_to_all.82 = bf16[8,512,64]{1,2,0:T(8,128)(2,1)} all-to-all(bf16[8,512,64]{1,2,0:T(8,128)(2,1)S(1)} %bitcast.118), channel_id=1, replica_groups=mesh['gen'=16,'tp'=8] {'tp'}, dimensions={0} | all-to-all | bytes 1048576 | tf_op jit(solution)/shard_map/all_to_all | solution.py:141
  54.8 0.0 all-gather.5.cloned.1.call-update
  54.8 1.3 fusion.59
  56.8 0.7 convert_element_type.97
  57.5 1.1 fusion.34
  58.7 0.2 fusion.36
  58.9 0.1 reshape.254
  59.0 0.1 add_convert_fusion.1
  59.1 0.1 copy.60
  59.2 0.1 multiply_cosine_fusion.1
  59.4 73.8 %all-gather.3.cloned.1.call-done = bf16[8192,768]{1,0:T(8,128)(2,1)} async-done(((bf16[512,768]{1,0:T(8,128)(2,1)}), bf16[8192,768]{1,0:T(8,128)(2,1)}) %all-gather.3.cloned.1.call-update) | async-done | bytes 12582928 | tf_op jit(solution)/shard_map/all_gather | solution.py:15
  133.2 4.7 %fusion.21 = f32[8,512]{1,0:T(8,128)S(1)} fusion(bf16[8,8192]{1,0:T(8,128)(2,1)S(1)} %reshape.254, bf16[8192,768]{1,0:T(8,128)(2,1)} %all-gather.3.cloned.1.call-done, f32[512]{0:T(512)S(1)} %convert_element_type.99), kind=kOutput, calls=%fused_computation.31 | convolution fusion | flops 67112960 | bytes 8538112 | tf_op jit(solution)/shard_map/dot_general | solution.py:143
  137.9 0.1 fusion.40
  138.0 0.1 maximum_bitcast_fusion
  138.1 2.0 fusion.24
  140.0 0.1 fusion.61
  140.1 0.1 fusion.47
  140.2 0.2 fusion.62
  140.5 2.0 fusion.31
  142.4 0.2 convolution_bitcast_fusion.1
  142.6 18.1 %while.14 = (s32[]{:T(128)}, f32[2,1,16]{2,0,1:T(2,128)S(1)}, f32[2,1,16]{2,0,1:T(2,128)S(1)}, f32[2,1,16,128]{3,2,0,1:T(8,128)S(1)}, s32[]{:T(128)}, /*index=5*...) while((s32[]{:T(128)}, f32[2,1,16]{2,0,1:T(2,128)S(1)}, ...), condition=%wide.region_7.8_spmd, body=%wide.region_4.7_spmd.sunk | while | flops 34027620 | bytes 2951359 | solution.py:98
  142.7 0.1 broadcast_compare_fusion.3
  142.7 1.8 fusion.78
  144.5 1.5 fusion.81
  146.1 0.2 fusion.80
  146.4 0.1 broadcast_compare_fusion.3
  146.4 1.7 fusion.78
  148.1 1.5 fusion.81
  149.7 0.2 fusion.80
  150.0 0.1 broadcast_compare_fusion.3
  150.0 1.7 fusion.78
  151.8 1.5 fusion.81
  153.3 0.2 fusion.80
  153.6 0.1 broadcast_compare_fusion.3
  153.7 1.7 fusion.78
  155.4 1.6 fusion.81
  156.9 0.2 fusion.80
  157.2 0.1 broadcast_compare_fusion.3
  157.3 1.7 fusion.78
  159.0 1.6 fusion.81
  160.5 0.2 fusion.80
  160.8 0.1 divide_convert_fusion
  160.9 45.1 %all-gather.5.cloned.1.call-done = bf16[512,8192]{0,1:T(8,128)(2,1)} async-done(((bf16[512,512]{0,1:T(8,128)(2,1)}), bf16[512,8192]{0,1:T(8,128)(2,1)}) %all-gather.5.cloned.1.call-update) | async-done | bytes 8388624 | tf_op jit(solution)/shard_map/all_gather | solution.py:169
  206.0 5.6 %convolution_convert_fusion = bf16[8,8192]{1,0:T(8,128)(2,1)S(1)} fusion(bf16[512,8192]{0,1:T(8,128)(2,1)} %all-gather.5.cloned.1.call-done, bf16[1,8,4,128]{3,2,1,0:T(4,128)(2,1)S(1)} %bitcast.128), kind=kOutput, calls=%fused_computation.22 | convolution fusion | flops 67174400 | bytes 8527872 | tf_op jit(solution)/shard_map/dot_general | solution.py:167
  211.6 1.1 broadcast_in_dim.37
  212.7 4.4 %all-to-all-start.4 = ((bf16[8,8,8192]{2,1,0:T(8,128)(2,1)}), bf16[8,8,8192]{2,1,0:T(8,128)(2,1)S(1)}, u32[]{:S(2)}, u32[]{:S(2)}) async-start(bf16[8,8,8192]{2,1,0:T(8,128)(2,1)} %broadcast_in_dim.37), calls=%async_computation.4 | async-start | bytes 2097152 | tf_op jit(solution)/shard_map/all_to_all | solution.py:21
  217.0 16.7 %all-to-all-done.4 = bf16[8,8,8192]{2,1,0:T(8,128)(2,1)S(1)} async-done(((bf16[8,8,8192]{2,1,0:T(8,128)(2,1)}), bf16[8,8,8192]{2,1,0:T(8,128)(2,1)S(1)}, u32[]{:S(2)}, u32[]{:S(2)}) %all-to-all-start.4) | async-done | bytes 1048608 | tf_op jit(solution)/shard_map/all_to_all | solution.py:21
  233.7 0.1 convert_reduce_fusion
  233.9 0.2 reshape.261
  234.0 0.9 fusion.37
  (45 shorter events, 0.3 us)
Async XLA Ops:
  6.5 1.0 copy-start
  6.5 52.5 %copy-start.3 = (s32[2]{0:T(128)S(1)}, s32[2]{0:T(128)}, u32[]{:S(2)}) copy-start(s32[2]{0:T(128)} %param.26) | copy-start | bytes 28
  6.5 52.2 %copy-start.1 = (bf16[4,2,8192]{2,1,0:T(2,128)(2,1)S(1)}, bf16[4,2,8192]{2,1,0:T(2,128)(2,1)}, u32[]{:S(2)}) copy-start(bf16[4,2,8192]{2,1,0:T(2,128)(2,1)} %param.15) | copy-start | bytes 393220
  6.5 52.4 %copy-start.2 = (bf16[512]{0:T(512)(128)(2,1)S(1)}, bf16[512]{0:T(512)(128)(2,1)}, u32[]{:S(2)}) copy-start(bf16[512]{0:T(512)(128)(2,1)} %param.20) | copy-start | bytes 3076
  6.5 52.6 %copy-start.5 = (bf16[128]{0:T(256)(128)(2,1)S(1)}, bf16[128]{0:T(256)(128)(2,1)}, u32[]{:S(2)}) copy-start(bf16[128]{0:T(256)(128)(2,1)} %param.21) | copy-start | bytes 772
  6.5 52.6 %copy-start.6 = (bf16[128]{0:T(256)(128)(2,1)S(1)}, bf16[128]{0:T(256)(128)(2,1)}, u32[]{:S(2)}) copy-start(bf16[128]{0:T(256)(128)(2,1)} %param.22) | copy-start | bytes 772
  8.2 12.3 %all-to-all-start.1 = ((bf16[64,8,128]{2,0,1:T(8,128)(2,1)}), bf16[64,8,128]{2,0,1:T(8,128)(2,1)S(1)}, u32[]{:S(2)}, u32[]{:S(2)}) async-start(bf16[64,8,128]{2,0,1:T(8,128)(2,1)} %copy_bitcast_fusion.3), calls=%async_computation.1 | async-start | bytes 262144 | tf_op jit(solution)/shard_map/all_to_all | solution.py:138
  20.5 9.7 %all-to-all-start.2 = ((bf16[64,8,128]{2,0,1:T(8,128)(2,1)}), bf16[64,8,128]{2,0,1:T(8,128)(2,1)S(1)}, u32[]{:S(2)}, u32[]{:S(2)}) async-start(bf16[64,8,128]{2,0,1:T(8,128)(2,1)} %copy_bitcast_fusion.2), calls=%async_computation.2 | async-start | bytes 262144 | tf_op jit(solution)/shard_map/all_to_all | solution.py:139
  23.9 109.2 %all-gather.3.cloned.1.call-start = ((), (), s32[]{:S(2)}) async-start(), calls=%async_computation.5 | async-start | bytes 13369344 | tf_op jit(solution)/shard_map/all_gather | solution.py:15
  42.3 163.7 %all-gather.5.cloned.1.call-start = ((), (), s32[]{:S(2)}) async-start(), calls=%async_computation.6 | async-start | bytes 8912896 | tf_op jit(solution)/shard_map/all_gather | solution.py:169
  160.8 56.3 %copy-start.4 = (s32[2]{0:T(128)S(1)}, s32[2]{0:T(128)}, u32[]{:S(2)}) copy-start(s32[2]{0:T(128)} %param.27) | copy-start | bytes 28
  212.7 21.1 %all-to-all-start.4 = ((bf16[8,8,8192]{2,1,0:T(8,128)(2,1)}), bf16[8,8,8192]{2,1,0:T(8,128)(2,1)S(1)}, u32[]{:S(2)}, u32[]{:S(2)}) async-start(bf16[8,8,8192]{2,1,0:T(8,128)(2,1)} %broadcast_in_dim.37), calls=%async_computation.4 | async-start | bytes 2097152 | tf_op jit(solution)/shard_map/all_to_all | solution.py:21
Sparse Core Ops, SparseCore 0:
  42.4 90.7 all-gather.2
  135.6 70.3 all-gather.4
where the time goes:
time: 243 us; the launch traced here: 242 us
  waiting for transfers between devices  146 us (60%)
  matrix products  31 us (13%)
  blocking collectives  22.4 us (9%)
  between operations  14.3 us (6%)
  starting transfers between devices  13.8 us (6%)
  other arithmetic  7.55 us (3%)
  local copies, waits for them, and re-layouts  6.9 us (3%)
    all_gather x1, waiting for transfers between devices, sent_together(): filled = lax.all_gather(both, axis, axis=dim, tiled=True)  73.8 us
    all_gather x1, waiting for transfers between devices, shards(): lax.all_gather(out_part, 'gen', axis=1, tiled=True)  45.1 us
    all_to_all x1, waiting for transfers between devices, from_everyone(): return lax.all_to_all(copies, axis, split_axis=0, concat_axis=0, tiled=True)  16.7 us
    all_to_all x1, blocking collectives, shards(): lax.all_to_all(w_out, 'tp', split_axis=0, concat_axis=1, tiled=True)  11.4 us
    all_to_all x1, blocking collectives, shards(): lax.all_to_all(w_query, 'tp', split_axis=1, concat_axis=0, tiled=True)  11 us
    dot_general x5, matrix products, visit(): jnp.einsum('rkqd,rkcd->rkqc', grouped_heads, key_block, preferred_element...  8.59 us
    dot_general x5, matrix products, visit(): jnp.einsum('rkqc,rkcd->rkqd', weights.astype(jnp.bfloat16), value_block,...  7.75 us
    all_to_all x1, starting transfers between devices, shards(): lax.all_to_all(key_weight_matrix, 'tp', split_axis=1, concat_axis=0, tile...  5.94 us
  transfers between devices with their start and end apart: 5, of which 5 were waited for; matrix products, arithmetic and copies ran while one was open for 14% of the time, Pallas kernels for 0%

commit v1 on v0

--- a/solution.py
+++ b/solution.py
@@ -166,7 +166,9 @@
     attended_flat = attended.reshape(step_count * row_count, query_heads * head_dim)
     partial_out = jnp.dot(
         attended_flat,
-        lax.all_gather(out_part, "gen", axis=1, tiled=True),
+        jnp.concatenate(
+            lax.all_to_all(jnp.stack([out_part] * lax.axis_size("gen")), "gen", 0, 0), axis=1
+        ),
         preferred_element_type=jnp.float32,
     )
     projected = of_everyone(partial_out.astype(jnp.bfloat16), "tp").astype(jnp.float32)

time: 243 us -> 292 us (1.20)
  the two profiles are of different devices: /device:TPU:0 before, /device:TPU:4 now
where the time goes in v1:
time: 292 us; the launch traced here: 291 us
  waiting for transfers between devices  182 us (62%)
  matrix products  37.4 us (13%)
  starting transfers between devices  24.2 us (8%)
  between operations  14.3 us (5%)
  local copies, waits for them, and re-layouts  11.7 us (4%)
  blocking collectives  11 us (4%)
  other arithmetic  9.79 us (3%)
    all_gather x1, waiting for transfers between devices, sent_together(): filled = lax.all_gather(both, axis, axis=dim, tiled=True)  153 us
    all_to_all x1, waiting for transfers between devices, from_everyone(): return lax.all_to_all(copies, axis, split_axis=0, concat_axis=0, tiled=True)  17.3 us
    dot_general x7, matrix products, visit(): jnp.einsum('rkqd,rkcd->rkqc', grouped_heads, key_block, preferred_element...  11.9 us
    all_to_all x1, blocking collectives, shards(): lax.all_to_all(w_query, 'tp', split_axis=1, concat_axis=0, tiled=True)  11 us
    dot_general x7, matrix products, visit(): jnp.einsum('rkqc,rkcd->rkqd', weights.astype(jnp.bfloat16), value_block,...  10.8 us
    all_to_all x1, starting transfers between devices, shards(): lax.all_to_all(jnp.stack([out_part] * lax.axis_size('gen')), 'gen', 0, 0)  7.91 us
  transfers between devices with their start and end apart: 6, of which 5 were waited for; matrix products, arithmetic and copies ran while one was open for 17% of the time, Pallas kernels for 0%

profile of v1, /device:TPU:4, one launch (start us, length us, event | category | flops | bytes accessed | tf_op | source)
XLA Modules:
  0.0 290.8 jit_solution(6526511319194498407)
XLA Ops:
  6.5 0.9 copy-done
  7.4 0.7 copy_bitcast_fusion.3
  8.1 5.8 %all-to-all-start.1 = ((bf16[64,8,128]{2,0,1:T(8,128)(2,1)}), bf16[64,8,128]{2,0,1:T(8,128)(2,1)S(1)}, u32[]{:S(2)}, u32[]{:S(2)}) async-start(bf16[64,8,128]{2,0,1:T(8,128)(2,1)} %copy_bitcast_fusion.3), calls=%async_computation.1 | async-start | bytes 262144 | tf_op jit(solution)/shard_map/all_to_all | solution.py:138
  13.9 1.6 copy_bitcast_fusion.2
  15.5 4.8 %all-to-all-done.1 = bf16[64,8,128]{2,0,1:T(8,128)(2,1)S(1)} async-done(((bf16[64,8,128]{2,0,1:T(8,128)(2,1)}), bf16[64,8,128]{2,0,1:T(8,128)(2,1)S(1)}, u32[]{:S(2)}, u32[]{:S(2)}) %all-to-all-start.1) | async-done | bytes 131104 | tf_op jit(solution)/shard_map/all_to_all | solution.py:138
  20.3 3.4 %all-to-all-start.2 = ((bf16[64,8,128]{2,0,1:T(8,128)(2,1)}), bf16[64,8,128]{2,0,1:T(8,128)(2,1)S(1)}, u32[]{:S(2)}, u32[]{:S(2)}) async-start(bf16[64,8,128]{2,0,1:T(8,128)(2,1)} %copy_bitcast_fusion.2), calls=%async_computation.2 | async-start | bytes 262144 | tf_op jit(solution)/shard_map/all_to_all | solution.py:139
  23.8 1.1 copy.94
  24.9 5.2 %all-to-all-done.2 = bf16[64,8,128]{2,0,1:T(8,128)(2,1)S(1)} async-done(((bf16[64,8,128]{2,0,1:T(8,128)(2,1)}), bf16[64,8,128]{2,0,1:T(8,128)(2,1)S(1)}, u32[]{:S(2)}, u32[]{:S(2)}) %all-to-all-start.2) | async-done | bytes 131104 | tf_op jit(solution)/shard_map/all_to_all | solution.py:139
  30.1 11.0 %all_to_all.83 = bf16[64,8,512]{2,0,1:T(8,128)(2,1)S(1)} all-to-all(bf16[64,8,512]{2,0,1:T(8,128)(2,1)S(1)} %bitcast.120), channel_id=1, replica_groups=mesh['gen'=16,'tp'=8] {'tp'}, dimensions={1} | all-to-all | bytes 1048576 | tf_op jit(solution)/shard_map/all_to_all | solution.py:137
  41.1 1.0 pad_maximum_fusion
  42.1 1.9 copy.93
  44.0 3.5 %all-to-all-start.3 = ((bf16[8,512,64]{1,2,0:T(8,128)(2,1)}), bf16[8,512,64]{1,2,0:T(8,128)(2,1)S(1)}, u32[]{:S(2)}, u32[]{:S(2)}) async-start(bf16[8,512,64]{1,2,0:T(8,128)(2,1)} %bitcast.100), calls=%async_computation.3 | async-start | bytes 1048576 | tf_op jit(solution)/shard_map/all_to_all | solution.py:141
  47.5 0.7 convert_element_type.97
  48.3 1.2 fusion.34
  49.4 0.7 add_convert_fusion.1
  50.1 1.3 fusion.59
  51.5 1.1 fusion.36
  53.3 0.1 copy.60
  53.5 0.1 multiply_cosine_fusion.1
  53.6 2.0 all-to-all-done.3
  55.6 4.1 %stack.5 = bf16[16,512,512]{1,2,0:T(8,128)(2,1)} broadcast(bf16[512,512]{0,1:T(8,128)(2,1)S(1)} %bitcast.118), dimensions={1,2} | broadcast | bytes 8912896 | tf_op jit(solution)/shard_map/stack | solution.py:170
  59.7 7.9 %all-to-all-start.4 = ((bf16[16,512,512]{1,2,0:T(8,128)(2,1)}), bf16[16,512,512]{1,2,0:T(8,128)(2,1)}, u32[]{:S(2)}, u32[]{:S(2)}) async-start(bf16[16,512,512]{1,2,0:T(8,128)(2,1)} %stack.5), calls=%async_computation.4 | async-start | bytes 16777216 | tf_op jit(solution)/shard_map/all_to_all | solution.py:170
  67.6 152.8 %all-gather.2.cloned.1.call-done = bf16[8192,768]{1,0:T(8,128)(2,1)} async-done(((bf16[512,768]{1,0:T(8,128)(2,1)}), bf16[8192,768]{1,0:T(8,128)(2,1)}) %all-gather.2.cloned.1.call-update) | async-done | bytes 12582928 | tf_op jit(solution)/shard_map/all_gather | solution.py:15
  220.4 4.7 %fusion.21 = f32[8,512]{1,0:T(8,128)S(1)} fusion(bf16[8,8192]{1,0:T(8,128)(2,1)S(1)} %reshape.263, bf16[8192,768]{1,0:T(8,128)(2,1)} %all-gather.2.cloned.1.call-done, f32[512]{0:T(512)S(1)} %convert_element_type.99), kind=kOutput, calls=%fused_computation.31 | convolution fusion | flops 67112960 | bytes 8538112 | tf_op jit(solution)/shard_map/dot_general | solution.py:143
  225.1 0.1 fusion.40
  225.2 2.0 fusion.24
  227.1 0.1 maximum_bitcast_fusion
  227.3 0.1 fusion.47
  227.4 0.2 fusion.62
  227.7 2.0 fusion.31
  229.6 0.2 convolution_bitcast_fusion.1
  229.8 25.2 %while.14 = (s32[]{:T(128)}, f32[2,1,16]{2,0,1:T(2,128)S(1)}, f32[2,1,16]{2,0,1:T(2,128)S(1)}, f32[2,1,16,128]{3,2,0,1:T(8,128)S(1)}, s32[]{:T(128)}, /*index=5*...) while((s32[]{:T(128)}, f32[2,1,16]{2,0,1:T(2,128)S(1)}, ...), condition=%wide.region_7.8_spmd, body=%wide.region_4.7_spmd.sunk | while | flops 34027620 | bytes 2951359 | solution.py:98
  229.8 0.1 broadcast_compare_fusion.3
  229.9 1.7 fusion.78
  231.7 1.5 fusion.81
  233.2 0.2 fusion.80
  233.6 1.7 fusion.78
  235.3 1.5 fusion.81
  236.8 0.2 fusion.80
  237.1 0.1 broadcast_compare_fusion.3
  237.2 1.7 fusion.78
  238.9 1.5 fusion.81
  240.4 0.2 fusion.80
  240.8 1.7 fusion.78
  242.5 1.5 fusion.81
  244.0 0.2 fusion.80
  244.3 0.1 broadcast_compare_fusion.3
  244.4 1.7 fusion.78
  246.1 1.5 fusion.81
  247.6 0.2 fusion.80
  247.9 0.1 broadcast_compare_fusion.3
  248.0 1.7 fusion.78
  249.7 1.5 fusion.81
  251.2 0.2 fusion.80
  251.6 1.7 fusion.78
  253.3 1.5 fusion.81
  254.8 0.2 fusion.80
  255.2 5.7 %convolution_convert_fusion = bf16[8,8192]{1,0:T(8,128)(2,1)S(1)} fusion(bf16[512,8192]{0,1:T(8,128)(2,1)} %bitcast.37, bf16[1,8,4,128]{3,2,1,0:T(4,128)(2,1)S(1)} %bitcast.130), kind=kOutput, calls=%fused_computation.22 | convolution fusion | flops 67174400 | bytes 8527872 | tf_op jit(solution)/shard_map/dot_general | solution.py:167
  260.9 1.1 broadcast_in_dim.37
  261.9 3.6 %all-to-all-start.5 = ((bf16[8,8,8192]{2,1,0:T(8,128)(2,1)}), bf16[8,8,8192]{2,1,0:T(8,128)(2,1)S(1)}, u32[]{:S(2)}, u32[]{:S(2)}) async-start(bf16[8,8,8192]{2,1,0:T(8,128)(2,1)} %broadcast_in_dim.37), calls=%async_computation.5 | async-start | bytes 2097152 | tf_op jit(solution)/shard_map/all_to_all | solution.py:21
  265.5 17.3 %all-to-all-done.5 = bf16[8,8,8192]{2,1,0:T(8,128)(2,1)S(1)} async-done(((bf16[8,8,8192]{2,1,0:T(8,128)(2,1)}), bf16[8,8,8192]{2,1,0:T(8,128)(2,1)S(1)}, u32[]{:S(2)}, u32[]{:S(2)}) %all-to-all-start.5) | async-done | bytes 1048608 | tf_op jit(solution)/shard_map/all_to_all | solution.py:21
  282.8 0.1 convert_reduce_fusion
  283.0 0.2 reshape.272
  283.1 0.9 fusion.37
  (60 shorter events, 0.9 us)
Async XLA Ops:
  6.5 0.9 copy-start
  6.5 46.8 %copy-start.2 = (bf16[512]{0:T(512)(128)(2,1)S(1)}, bf16[512]{0:T(512)(128)(2,1)}, u32[]{:S(2)}) copy-start(bf16[512]{0:T(512)(128)(2,1)} %param.20) | copy-start | bytes 3076
  6.5 46.9 %copy-start.4 = (bf16[128]{0:T(256)(128)(2,1)S(1)}, bf16[128]{0:T(256)(128)(2,1)}, u32[]{:S(2)}) copy-start(bf16[128]{0:T(256)(128)(2,1)} %param.21) | copy-start | bytes 772
  6.5 46.9 %copy-start.5 = (bf16[128]{0:T(256)(128)(2,1)S(1)}, bf16[128]{0:T(256)(128)(2,1)}, u32[]{:S(2)}) copy-start(bf16[128]{0:T(256)(128)(2,1)} %param.22) | copy-start | bytes 772
  8.1 12.2 %all-to-all-start.1 = ((bf16[64,8,128]{2,0,1:T(8,128)(2,1)}), bf16[64,8,128]{2,0,1:T(8,128)(2,1)S(1)}, u32[]{:S(2)}, u32[]{:S(2)}) async-start(bf16[64,8,128]{2,0,1:T(8,128)(2,1)} %copy_bitcast_fusion.3), calls=%async_computation.1 | async-start | bytes 262144 | tf_op jit(solution)/shard_map/all_to_all | solution.py:138
  20.3 9.7 %all-to-all-start.2 = ((bf16[64,8,128]{2,0,1:T(8,128)(2,1)}), bf16[64,8,128]{2,0,1:T(8,128)(2,1)S(1)}, u32[]{:S(2)}, u32[]{:S(2)}) async-start(bf16[64,8,128]{2,0,1:T(8,128)(2,1)} %copy_bitcast_fusion.2), calls=%async_computation.2 | async-start | bytes 262144 | tf_op jit(solution)/shard_map/all_to_all | solution.py:139
  23.7 196.6 %all-gather.2.cloned.1.call-start = ((), (), s32[]{:S(2)}) async-start(), calls=%async_computation.6 | async-start | bytes 13369344 | tf_op jit(solution)/shard_map/all_gather | solution.py:15
  44.0 11.6 %all-to-all-start.3 = ((bf16[8,512,64]{1,2,0:T(8,128)(2,1)}), bf16[8,512,64]{1,2,0:T(8,128)(2,1)S(1)}, u32[]{:S(2)}, u32[]{:S(2)}) async-start(bf16[8,512,64]{1,2,0:T(8,128)(2,1)} %bitcast.100), calls=%async_computation.3 | async-start | bytes 1048576 | tf_op jit(solution)/shard_map/all_to_all | solution.py:141
  59.7 195.5 %all-to-all-start.4 = ((bf16[16,512,512]{1,2,0:T(8,128)(2,1)}), bf16[16,512,512]{1,2,0:T(8,128)(2,1)}, u32[]{:S(2)}, u32[]{:S(2)}) async-start(bf16[16,512,512]{1,2,0:T(8,128)(2,1)} %stack.5), calls=%async_computation.4 | async-start | bytes 16777216 | tf_op jit(solution)/shard_map/all_to_all | solution.py:170
  255.1 10.4 %copy-start.3 = (s32[2]{0:T(128)S(1)}, s32[2]{0:T(128)}, u32[]{:S(2)}) copy-start(s32[2]{0:T(128)} %param.27) | copy-start | bytes 28
  255.2 27.9 %copy-start.1 = (bf16[4,2,8192]{2,1,0:T(2,128)(2,1)S(1)}, bf16[4,2,8192]{2,1,0:T(2,128)(2,1)}, u32[]{:S(2)}) copy-start(bf16[4,2,8192]{2,1,0:T(2,128)(2,1)} %param.15) | copy-start | bytes 393220
  261.9 20.9 %all-to-all-start.5 = ((bf16[8,8,8192]{2,1,0:T(8,128)(2,1)}), bf16[8,8,8192]{2,1,0:T(8,128)(2,1)S(1)}, u32[]{:S(2)}, u32[]{:S(2)}) async-start(bf16[8,8,8192]{2,1,0:T(8,128)(2,1)} %broadcast_in_dim.37), calls=%async_computation.5 | async-start | bytes 2097152 | tf_op jit(solution)/shard_map/all_to_all | solution.py:21
Sparse Core Ops, SparseCore 0:
  42.2 178.0 all-gather.1
